TPU v7x, 256 devices: a whole 4x4x8 slice. The times are simulated.
256 devices in a mesh: seq: 32 (over y, z), head: 8 (over x, core).
Axes of the slice: x: 4, y: 4, z: 8, core: 2. Of those that a mesh axis runs over, the one named last changes fastest.
Arguments:
- tokens: bfloat16 [24576, 2560], P(('seq', 'head')), may hold values from -12 to 12
- pre_gain: float32 [2560], replicated, may hold values from 0.25 to 1.75
- inner_proj: bfloat16 [2560, 2, 5120], P(None, None, 'head'), may hold values from -0.125 to 0.125
- outer_proj: bfloat16 [2560, 336], replicated, may hold values from -0.125 to 0.125
- kernel_x: float32 [4, 5120], P(None, 'head'), may hold values from -3 to 3
- kernel_bc: float32 [4, 256], replicated, may hold values from -3 to 3
- offset_x: float32 [5120], P('head'), may hold values from -3 to 3
- offset_bc: float32 [256], replicated, may hold values from -3 to 3
- dt_bias: float32 [80], P('head'), may hold values from -7 to -5
- a_log: float32 [80], P('head'), may hold values from -12 to 4
- skip_gain: float32 [80], P('head'), may hold values from 0.5 to 1.5
- norm_gain: float32 [5120], P('head'), may hold values from 0.25 to 1.75
- out_proj: bfloat16 [5120, 2560], P('head'), may hold values from -0.078125 to 0.078125
Outputs:
- mixed: bfloat16 [24576, 2560], P(('seq', 'head'))
All inputs are finite; a program needn't handle non-finite values.
Results may differ from a plain program's by a relative error of at most 0.014.
Values may be sent and summed in bfloat16 or wider, within the bound.
A program may use at most 128 MiB of HBM per device.

v0:
```python
import jax
import jax.numpy as jnp
from jax import lax
from jax.sharding import Mesh
from jax.sharding import PartitionSpec as P

SPAN = 256
SEQ = ("seq_0", "seq_1")
SEQ_HEAD = ("seq_0", "seq_1", "head")
norm_floor = 0.1


def passed_along(block, axis, distance):
    devices = range(lax.axis_size(axis))
    route = [(i - distance, i) for i in devices if i - distance in devices]
    return lax.ppermute(block, axis, route)


def nothing_yet(array, identity):
    return jax.tree.map(
        lambda part, zero: jnp.zeros_like(part) + jnp.asarray(zero, part.dtype), array, identity
    )


def entering(array, axes, combine, identity):
    before = start = nothing_yet(array, identity)
    subtotal = array
    for axis in reversed(axes):
        length, position = (lax.axis_size(axis), lax.axis_index(axis))
        pieces = jax.tree.map(
            lambda part, kind: lax.all_gather(part.astype(kind), axis),
            subtotal,
            (jnp.bfloat16, jnp.bfloat16),
        )
        inside, subtotal = (start, start)
        for k in range(length):
            passed = k < position
            subtotal = combine(
                subtotal, jax.tree.map(lambda part, own: part[k].astype(own.dtype), pieces, array)
            )
            inside = jax.tree.map(lambda new, old: jnp.where(passed, new, old), subtotal, inside)
        before = combine(inside, before)
    return before


def from_everyone(array, axis):
    length = lax.axis_size(axis)
    return lax.all_to_all(
        jnp.broadcast_to(array[None], (length, *array.shape)), axis, 0, 0, tiled=True
    )


def taken_together(array, axis):
    everything = from_everyone(array, axis)
    return jnp.sum(everything, axis=0)


def cut_along(array, dim, length):
    before, after = (array.shape[:dim], array.shape[dim + 1 :])
    return jnp.moveaxis(array.reshape(*before, length, -1, *after), dim, 0)


def summed_on_arrival(array, axis, dim):
    pieces = cut_along(array, dim, lax.axis_size(axis))
    arrived = lax.all_to_all(pieces, axis, split_axis=0, concat_axis=0, tiled=True)
    return arrived.astype(jnp.float32).sum(axis=0)


def row_norm(row_block, gain_vector):
    widened = row_block.astype(jnp.float32)
    inverse_rms = lax.rsqrt(jnp.mean(widened * widened, axis=-1, keepdims=True) + norm_floor)
    return widened * inverse_rms * gain_vector


def masked_exp(log_gap, causal):
    return jnp.where(causal, jnp.exp(jnp.where(causal, log_gap, 0.0)), 0.0)


def on_device(
    tokens,
    pre_gain,
    inner_proj,
    outer_proj,
    kernel_x,
    kernel_bc,
    offset_x,
    offset_bc,
    dt_bias,
    a_log,
    skip_gain,
    norm_gain,
    out_proj,
):
    model_width = inner_proj.shape[0]
    local_width = inner_proj.shape[2]
    head_count = dt_bias.shape[0]
    head_size = local_width // head_count
    state_size = kernel_bc.shape[1] // 2
    kernel_size = kernel_x.shape[0]
    joined_proj = inner_proj.reshape(model_width, 2 * local_width)
    own_normed = row_norm(tokens, pre_gain).astype(jnp.bfloat16)
    normed = lax.all_gather(own_normed, "head", axis=0, tiled=True)
    inner_part = jnp.dot(normed, joined_proj, preferred_element_type=jnp.float32)
    outer_part = jnp.dot(normed, outer_proj, preferred_element_type=jnp.float32)
    projected = jnp.concatenate([inner_part, outer_part], axis=1)
    seq_rows = projected.shape[0]
    gate_in = projected[:, :local_width].astype(jnp.bfloat16)
    conv_input = projected[:, local_width : 2 * local_width + 2 * state_size].astype(jnp.bfloat16)
    head_index = lax.axis_index("head")
    dt_raw = lax.dynamic_slice_in_dim(
        projected[:, 2 * local_width + 2 * state_size :], head_index * head_count, head_count, 1
    )
    conv_tail = passed_along(conv_input[seq_rows - kernel_size + 1 :], SEQ, 1)
    extended = jnp.concatenate([conv_tail, conv_input], axis=0)
    conv_weight = jnp.concatenate([kernel_x, kernel_bc], axis=1)
    conv_bias = jnp.concatenate([offset_x, offset_bc])
    summed = jnp.broadcast_to(conv_bias, conv_input.shape)
    for offset in range(kernel_size):
        summed = summed + conv_weight[offset] * extended[offset : offset + seq_rows].astype(
            jnp.float32
        )
    conv_out = jax.nn.silu(summed).astype(jnp.bfloat16)
    blocks = seq_rows // SPAN
    values_x = conv_out[:, :local_width].reshape(blocks, SPAN, head_count, head_size)
    values_b = conv_out[:, local_width : local_width + state_size].reshape(blocks, SPAN, state_size)
    values_c = conv_out[:, local_width + state_size :].reshape(blocks, SPAN, state_size)
    step_flat = jax.nn.softplus(dt_raw + dt_bias)
    log_rates = (step_flat * -jnp.exp(a_log)).reshape(blocks, SPAN, head_count)
    step_sizes = step_flat.reshape(blocks, SPAN, head_count)
    running = jnp.cumsum(log_rates, axis=1)
    score_rows = jnp.einsum("ctn,csn->cts", values_c, values_b, preferred_element_type=jnp.float32)
    running_heads = jnp.transpose(running, (0, 2, 1))
    steps_heads = jnp.transpose(step_sizes, (0, 2, 1))
    row_index = lax.broadcasted_iota(jnp.int32, (SPAN, SPAN), 0)
    col_index = lax.broadcasted_iota(jnp.int32, (SPAN, SPAN), 1)
    decay_factor = masked_exp(
        running_heads[:, :, :, None] - running_heads[:, :, None, :], row_index >= col_index
    )
    mix_weights = (score_rows[:, None] * decay_factor * steps_heads[:, :, None, :]).astype(
        jnp.bfloat16
    )
    intra_out = jnp.einsum(
        "chts,cshp->cthp", mix_weights, values_x, preferred_element_type=jnp.float32
    )
    end_weight = jnp.exp(running[:, -1:, :] - running) * step_sizes
    scaled_x = (values_x.astype(jnp.float32) * end_weight[..., None]).astype(jnp.bfloat16)
    block_states = jnp.einsum(
        "cshp,csn->chpn", scaled_x, values_b, preferred_element_type=jnp.float32
    )
    block_total = running[:, -1, :]
    prefix_rate = jnp.concatenate(
        [jnp.zeros((1, head_count), jnp.float32), jnp.cumsum(block_total, axis=0)], axis=0
    )
    prefix_heads = prefix_rate.T
    later_index = lax.broadcasted_iota(jnp.int32, (blocks + 1, blocks), 0)
    source_index = lax.broadcasted_iota(jnp.int32, (blocks + 1, blocks), 1)
    link_weight = masked_exp(
        prefix_heads[:, :, None] - prefix_heads[:, None, 1:], source_index < later_index
    )
    local_states = jnp.einsum(
        "hce,ehpn->chpn", link_weight, block_states, precision=lax.Precision.HIGHEST
    )
    summary = local_states[blocks]
    device_rate = prefix_rate[blocks]

    def combine(earlier_part, later_part):
        return (
            earlier_part[0] + later_part[0],
            jnp.exp(later_part[0])[:, None, None] * earlier_part[1] + later_part[1],
        )

    identity = (
        jnp.zeros((head_count,), jnp.float32),
        jnp.zeros((head_count, head_size, state_size), jnp.float32),
    )
    carried = entering((device_rate, summary), SEQ, combine, identity)[1]
    block_inputs = (
        local_states[:blocks] + jnp.exp(prefix_rate[:blocks])[:, :, None, None] * carried[None]
    )
    cross_out = jnp.exp(running)[..., None] * jnp.einsum(
        "ctn,chpn->cthp",
        values_c.astype(jnp.float32),
        block_inputs,
        precision=lax.Precision.HIGHEST,
    )
    mixer_out = (intra_out + cross_out + skip_gain[:, None] * values_x.astype(jnp.float32)).reshape(
        seq_rows, local_width
    )
    gated = mixer_out * jax.nn.silu(gate_in.astype(jnp.float32))
    squares = taken_together(jnp.sum(gated * gated, axis=1), "head")
    inverse_rms = lax.rsqrt(squares / (local_width * lax.axis_size("head")) + norm_floor)
    normed_out = (gated * inverse_rms[:, None] * norm_gain).astype(jnp.bfloat16)
    mixed = summed_on_arrival(
        jnp.dot(normed_out, out_proj, preferred_element_type=jnp.float32).astype(jnp.bfloat16),
        "head",
        0,
    )
    return mixed.astype(jnp.bfloat16)


def solution(mesh):
    finer = Mesh(mesh.devices.reshape(4, 8, mesh.shape["head"]), ("seq_0", "seq_1", "head"))
    in_specs = (
        P(SEQ_HEAD, None),
        P(),
        P(None, None, "head"),
        P(),
        P(None, "head"),
        P(),
        P("head"),
        P(),
        P("head"),
        P("head"),
        P("head"),
        P("head"),
        P("head", None),
    )
    out_specs = P(SEQ_HEAD, None)
    return jax.shard_map(
        on_device, mesh=finer, in_specs=in_specs, out_specs=out_specs, check_vma=False
    )
```

profile of v0, /device:TPU:1, one launch (start us, length us, event | category | flops | bytes accessed | tf_op | source)
XLA Modules:
  0.0 240.8 jit_solution(7252940572213324971)
XLA Ops:
  6.5 1.4 fusion.16
  7.9 2.0 fusion.18
  10.1 6.7 %copy.137 = bf16[320,8,2,640]{3,1,2,0:T(8,128)(2,1)} copy(bf16[320,8,2,640]{3,2,1,0:T(2,128)(2,1)} %bitcast.167) | data formatting | bytes 13107200
  18.1 29.7 %all-gather.5.cloned.1.call-done = bf16[768,2560]{1,0:T(8,128)(2,1)} async-done(((bf16[96,2560]{1,0:T(8,128)(2,1)}), bf16[768,2560]{1,0:T(8,128)(2,1)}) %all-gather.5.cloned.1.call-update) | async-done | bytes 3932176 | tf_op jit(solution)/shard_map/all_gather | solution.py:102
  47.8 5.3 %fusion.66 = (bf16[768,336]{0,1:T(8,128)(2,1)}, f32[768,336]{0,1:T(8,128)}) fusion(bf16[768,2560]{1,0:T(8,128)(2,1)} %all-gather.5.cloned.1.call-done, bf16[2560,336]{0,1:T(8,128)(2,1)} %param.16), kind=kOutput, calls=%fused_computation.144 | convolution fusion | flops 1321463808 | bytes 7200768 | tf_op jit(solution)/shard_map/dot_general | solution.py:104
  53.1 2.1 copy.111
  55.2 8.9 %convolution_convert_fusion.1 = bf16[768,1280]{1,0:T(8,128)(2,1)S(1)} fusion(bf16[768,2560]{1,0:T(8,128)(2,1)} %all-gather.5.cloned.1.call-done, bf16[2560,1280]{1,0:T(8,128)(2,1)} %bitcast.168), kind=kOutput, calls=%fused_computation.9 | convolution fusion | flops 5034147840 | bytes 12451840 | tf_op jit(solution)/shard_map/dot_general | solution.py:103
  64.2 1.3 pad_maximum_fusion.1
  66.5 1.0 slice.213
  67.6 1.7 reduce-window.6
  70.1 3.2 %collective-permute-start = (bf16[3,896]{1,0:T(4,128)(2,1)}, bf16[3,896]{1,0:T(4,128)(2,1)S(1)}, u32[]{:S(2)}, u32[]{:S(2)}) collective-permute-start(bf16[3,896]{1,0:T(4,128)(2,1)} %pad_maximum_fusion.2), channel_id=1, source_target_pairs={{0,8},{8,16},{16,24},{24,32},{32,40},{40,48},{48,56},{56,64},{64,7... | collective-permute-start | bytes 16136 | tf_op jit(solution)/shard_map/ppermute | solution.py:16
  73.3 0.6 bitcast_exponential_fusion
  73.9 0.7 copy.124
  74.6 0.6 copy.123
  75.2 0.7 copy.125
  75.9 5.0 %multiply_convert_fusion.2 = bf16[768,896]{1,0:T(8,128)(2,1)S(1)} fusion(bf16[768,896]{1,0:T(8,128)(2,1)} %pad_maximum_fusion.1, bf16[3,896]{1,0:T(4,128)(2,1)S(1)} %collective-permute-done, f32[896]{0:T(1024)S(1)} %get-tuple-element.6, f32[896]{0:T(1024)S(1)} %get-tuple-element.7, f32[896]{0:T(1024)S(1)} %get-tuple-element.8, f32[896]{0:T(1024)S(1)} %get-tuple-element.5, ...), kind=kLoop, calls=%fused_computation.10 | loop fusion | flops 17891328 | bytes 2775808 | tf_op jit(solution)/shard_map/convert_element_type | solution.py:122
  80.9 0.7 fusion.65
  81.6 1.1 slice.210
  82.6 2.3 copy.112
  84.9 3.8 %reshape.237 = bf16[3,256,10,64]{1,0,3,2:T(4,128)(2,1)} reshape(bf16[768,640]{0,1:T(8,128)(2,1)} %copy.112) | data formatting | bytes 1966080 | tf_op jit(solution)/shard_map/reshape | solution.py:124
  88.7 1.8 fusion.19
  90.5 2.8 %convolution_bitcast_fusion = f32[4,10,64,128]{3,0,2,1:T(4,128)S(1)} fusion(f32[3,10,64,128]{3,2,1,0:T(8,128)S(1)} %fusion.19, f32[10,3]{1,0:T(8,128)S(1)} %copy-done.14, f32[10,4]{1,0:T(8,128)S(1)} %copy-done.13, pred[4,3]{1,0:T(4,128)(4,1)S(1)} %copy-done.27), kind=kOutput, calls=%fused_computation.26 | convolution fusion | flops 11796840 | bytes 2294052 | tf_op jit(solution)/shard_map/hce,ehpn->chpn/dot_general | solution.py:160
  93.4 1.1 copy-done.2
  94.8 0.7 copy.128
  95.5 0.6 iota_compare_fusion
  96.2 1.4 slice_exponential_fusion
  97.5 12.2 %all-gather = bf16[8,1,10]{2,1,0:T(2,128)(2,1)S(1)} all-gather(bf16[1,1,10]{2,1,0:T(2,128)(2,1)S(1)} %slice_bitcast_fusion.5), channel_id=1, replica_groups=mesh['seq_0'=4,'seq_1'=8,'head'=8] {'seq_1'}, dimensions={0}, use_global_device_ids=true | all-gather | bytes 180 | tf_op jit(solution)/shard_map/all_gather | solution.py:31
  110.9 8.6 %all-gather.1 = bf16[4,1,10]{2,1,0:T(2,128)(2,1)} all-gather(bf16[1,1,10]{2,1,0:T(2,128)(2,1)S(1)} %get-tuple-element.17), channel_id=1, replica_groups=mesh['seq_0'=4,'seq_1'=8,'head'=8] {'seq_0'}, dimensions={0}, use_global_device_ids=true | all-gather | bytes 100 | tf_op jit(solution)/shard_map/all_gather | solution.py:31
  119.5 0.6 copy.115
  120.2 0.8 copy.127
  120.9 1.4 copy.119
  122.3 0.6 copy.117
  123.6 0.7 fusion.49
  124.3 2.1 fusion.67
  126.4 4.1 %all-gather.7.cloned.1.call-done = bf16[8,10,64,128]{3,2,1,0:T(8,128)(2,1)} async-done(((bf16[1,10,64,128]{3,2,1,0:T(8,128)(2,1)}), bf16[8,10,64,128]{3,2,1,0:T(8,128)(2,1)}) %all-gather.7.cloned.1.call-update) | async-done | bytes 1310736 | tf_op jit(solution)/shard_map/all_gather | solution.py:31
  130.4 1.9 fusion.28
  132.3 10.4 %all_gather.23 = bf16[4,10,64,128]{3,2,1,0:T(8,128)(2,1)S(1)} all-gather(bf16[1,10,64,128]{3,2,1,0:T(8,128)(2,1)S(1)} %fusion.28), channel_id=1, replica_groups=mesh['seq_0'=4,'seq_1'=8,'head'=8] {'seq_0'}, dimensions={0}, use_global_device_ids=true | all-gather | bytes 819200 | tf_op jit(solution)/shard_map/all_gather | solution.py:31
  142.8 1.0 add_bitcast_fusion
  144.3 0.9 fusion.21
  145.7 2.7 %fusion.8 = f32[3,256,10,64]{1,3,2,0:T(8,128)S(1)} fusion(f32[3,256,10,64]{1,3,2,0:T(8,128)S(1)} %fusion.21, f32[3,10,256]{2,1,0:T(8,128)S(1)} %copy-done.11, f32[3,10,256]{2,1,0:T(8,128)S(1)} %copy-done.9, f32[3,256,256]{2,1,0:T(8,128)S(1)} %copy-done.7, pred[256,256]{1,0:T(8,128)(4,1)S(1)} %copy-done.8, f32[10]{0:T(128)S(1)} %copy-done.30, ...), kind=kOutput, calls=%fused_computation.16 | convolution fusion | flops 265912320 | bytes 5859368 | tf_op jit(solution)/shard_map/chts,cshp->cthp/dot_general | solution.py:142
  148.4 1.4 copy.130
  149.8 1.8 copy.138
  151.6 2.8 %copy.131 = f32[768,640]{1,0:T(8,128)} copy(f32[768,640]{0,1:T(8,128)} %bitcast.166) | data formatting | bytes 3932160 | tf_op jit(solution)/shard_map/reshape | solution.py:186
  154.4 2.5 %multiply_reduce_fusion = f32[768]{0:T(1024)S(1)} fusion(f32[768,640]{1,0:T(8,128)} %copy.131, bf16[768,1280]{1,0:T(8,128)(2,1)} %copy-done.1), kind=kLoop, calls=%fused_computation.23 | loop fusion | flops 3931392 | bytes 2952192 | tf_op jit(solution)/shard_map/reduce_sum | solution.py:190
  156.9 17.4 %all_to_all.11 = f32[8,1,768]{2,1,0:T(1,128)S(1)} all-to-all(f32[8,1,768]{2,1,0:T(1,128)S(1)} %broadcast_in_dim.36), channel_id=1, replica_groups=mesh['seq_0'=4,'seq_1'=8,'head'=8] {'head'}, dimensions={0} | all-to-all | bytes 49152 | tf_op jit(solution)/shard_map/all_to_all | solution.py:48
  174.4 6.2 %convolution_convert_fusion = bf16[768,2560]{1,0:T(8,128)(2,1)S(1)} fusion(bf16[640,2560]{1,0:T(8,128)(2,1)S(1)} %copy-done, f32[640]{0:T(1024)S(1)} %copy-done.28, f32[768]{0:T(1024)S(1)} %add_rsqrt_fusion, f32[768,640]{1,0:T(8,128)} %copy.131, bf16[768,1280]{1,0:T(8,128)(2,1)} %copy-done.1), kind=kOutput, calls=%fused_computation.1 | convolution fusion | flops 2522972160 | bytes 10163712 | tf_op jit(solution)/shard_map/dot_general | solution.py:194
  180.6 49.8 %all_to_all.12 = bf16[8,96,2560]{2,1,0:T(8,128)(2,1)} all-to-all(bf16[8,96,2560]{2,1,0:T(8,128)(2,1)S(1)} %bitcast.169), channel_id=1, replica_groups=mesh['seq_0'=4,'seq_1'=8,'head'=8] {'head'}, dimensions={0} | all-to-all | bytes 7864320 | tf_op jit(solution)/shard_map/all_to_all | solution.py:65
  230.4 3.6 %reduce_sum.42 = bf16[96,2560]{1,0:T(8,128)(2,1)} reduce(bf16[8,96,2560]{2,1,0:T(8,128)(2,1)} %all_to_all.12, bf16[]{:T(256)} %constant.60.clone.1), dimensions={0}, to_apply=%region_6.7 | reduce | flops 1720320 | bytes 4423682 | tf_op jit(solution)/shard_map/reduce_sum | solution.py:66
  (100 shorter events, 6.4 us)
Async XLA Ops:
  6.5 167.9 %copy-start = (bf16[640,2560]{1,0:T(8,128)(2,1)S(1)}, bf16[640,2560]{1,0:T(8,128)(2,1)}, u32[]{:S(2)}) copy-start(bf16[640,2560]{1,0:T(8,128)(2,1)} %param.25) | copy-start | bytes 9830404
  6.5 41.2 %all-gather.5.cloned.1.call-start = ((), (), s32[]{:S(2)}) async-start(), calls=%async_computation.2 | async-start | bytes 4423680 | tf_op jit(solution)/shard_map/all_gather | solution.py:102
  10.0 120.5 %all-gather.7.cloned.1.call-start = ((), (), s32[]{:S(2)}) async-start(), calls=%async_computation.3 | async-start | bytes 1474560 | tf_op jit(solution)/shard_map/all_gather | solution.py:31
  10.0 7.4 %copy-start.16 = (f32[4,640]{1,0:T(4,128)S(1)}, f32[4,640]{1,0:T(4,128)}, u32[]{:S(2)}) copy-start(f32[4,640]{1,0:T(4,128)} %param.17) | copy-start | bytes 30724
  10.0 7.4 %copy-start.22 = (f32[4,256]{1,0:T(4,128)S(1)}, f32[4,256]{1,0:T(4,128)}, u32[]{:S(2)}) copy-start(f32[4,256]{1,0:T(4,128)} %param.18) | copy-start | bytes 12292
  10.0 7.4 %copy-start.23 = (f32[640]{0:T(1024)S(1)}, f32[640]{0:T(1024)}, u32[]{:S(2)}) copy-start(f32[640]{0:T(1024)} %param.19) | copy-start | bytes 7684
  10.1 7.4 %copy-start.25 = (f32[256]{0:T(256)S(1)}, f32[256]{0:T(256)}, u32[]{:S(2)}) copy-start(f32[256]{0:T(256)} %param.20) | copy-start | bytes 3076
  10.1 8.0 %copy-start.29 = (f32[10]{0:T(128)S(1)}, f32[10]{0:T(128)}, u32[]{:S(2)}) copy-start(f32[10]{0:T(128)} %param.22) | copy-start | bytes 124
  55.2 8.9 %copy-start.4 = (bf16[768,336]{1,0:T(8,128)(2,1)S(1)}, bf16[768,336]{1,0:T(8,128)(2,1)}, u32[]{:S(2)}) copy-start(bf16[768,336]{1,0:T(8,128)(2,1)} %copy.111) | copy-start | bytes 1548292
  64.2 1.7 copy-start.1
  65.9 1.6 copy-start.26
  70.0 5.9 %copy-start.15 = (f32[3,10]{1,0:T(4,128)}, f32[3,10]{1,0:T(4,128)S(1)}, u32[]{:S(2)}) copy-start(f32[3,10]{1,0:T(4,128)S(1)} %reduce_window_sum.36) | copy-start | bytes 364
  70.1 5.8 %collective-permute-start = (bf16[3,896]{1,0:T(4,128)(2,1)}, bf16[3,896]{1,0:T(4,128)(2,1)S(1)}, u32[]{:S(2)}, u32[]{:S(2)}) collective-permute-start(bf16[3,896]{1,0:T(4,128)(2,1)} %pad_maximum_fusion.2), channel_id=1, source_target_pairs={{0,8},{8,16},{16,24},{24,32},{32,40},{40,48},{48,56},{56,64},{64,7... | collective-permute-start | bytes 16136 | tf_op jit(solution)/shard_map/ppermute | solution.py:16
  88.7 1.8 copy-start.13
  88.7 1.8 copy-start.14
  88.7 1.8 copy-start.27
  93.4 1.1 copy-start.2
  109.7 10.4 %copy-start.12 = (bf16[8,1,10]{2,1,0:T(2,128)(2,1)}, bf16[8,1,10]{2,1,0:T(2,128)(2,1)S(1)}, u32[]{:S(2)}) copy-start(bf16[8,1,10]{2,1,0:T(2,128)(2,1)S(1)} %all-gather) | copy-start | bytes 484
  120.1 22.6 %copy-start.17 = (f32[10]{0:T(128)S(1)}, f32[10]{0:T(128)}, u32[]{:S(2)}) copy-start(f32[10]{0:T(128)} %get-tuple-element.18) | copy-start | bytes 124
  120.1 22.6 %copy-start.18 = (f32[10]{0:T(128)S(1)}, f32[10]{0:T(128)}, u32[]{:S(2)}) copy-start(f32[10]{0:T(128)} %get-tuple-element.19) | copy-start | bytes 124
  120.1 22.6 %copy-start.19 = (f32[10]{0:T(128)S(1)}, f32[10]{0:T(128)}, u32[]{:S(2)}) copy-start(f32[10]{0:T(128)} %get-tuple-element.20) | copy-start | bytes 124
  120.1 22.6 %copy-start.20 = (f32[10]{0:T(128)S(1)}, f32[10]{0:T(128)}, u32[]{:S(2)}) copy-start(f32[10]{0:T(128)} %get-tuple-element.21) | copy-start | bytes 124
  120.2 22.6 %copy-start.21 = (f32[10]{0:T(128)S(1)}, f32[10]{0:T(128)}, u32[]{:S(2)}) copy-start(f32[10]{0:T(128)} %get-tuple-element.22) | copy-start | bytes 124
  123.0 19.8 %copy-start.24 = (f32[10]{0:T(128)S(1)}, f32[10]{0:T(128)}, u32[]{:S(2)}) copy-start(f32[10]{0:T(128)} %get-tuple-element.9) | copy-start | bytes 124
  130.4 12.3 %copy-start.5 = (bf16[8,10,64,128]{3,2,1,0:T(8,128)(2,1)S(1)}, bf16[8,10,64,128]{3,2,1,0:T(8,128)(2,1)}, u32[]{:S(2)}) copy-start(bf16[8,10,64,128]{3,2,1,0:T(8,128)(2,1)} %all-gather.7.cloned.1.call-done) | copy-start | bytes 3932164
  130.4 13.3 %copy-start.3 = (f32[4,10,64,128]{3,0,2,1:T(4,128)S(1)}, f32[4,10,64,128]{3,0,2,1:T(4,128)}, u32[]{:S(2)}) copy-start(f32[4,10,64,128]{3,0,2,1:T(4,128)} %copy-done.2) | copy-start | bytes 3932164
  144.2 1.3 copy-start.6
  144.2 1.5 copy-start.7
  144.2 1.5 copy-start.8
  144.2 1.5 copy-start.9
  144.2 1.5 copy-start.10
  144.2 1.5 copy-start.11
  144.2 1.5 copy-start.30
  154.4 20.0 %copy-start.28 = (f32[640]{0:T(1024)S(1)}, f32[640]{0:T(1024)}, u32[]{:S(2)}) copy-start(f32[640]{0:T(1024)} %param.24) | copy-start | bytes 7684
Sparse Core Ops, SparseCore 0:
  10.1 37.6 all-gather.4
  95.6 34.7 all-gather.6
where the time goes:
time: 242 us; the launch traced here: 241 us
  blocking collectives  98.4 us (41%)
  waiting for transfers between devices  33.8 us (14%)
  local copies, waits for them, and re-layouts  32.7 us (14%)
  matrix products  30.8 us (13%)
  other arithmetic  28 us (12%)
  between operations  13.9 us (6%)
  starting transfers between devices  3.23 us (1%)
    all_to_all x1, blocking collectives, summed_on_arrival(): lax.all_to_all(pieces, axis, split_axis=0, concat_axis=0, tiled=True)  49.8 us
    all_gather x3, blocking collectives, entering(): lax.all_gather(part.astype(kind), axis)  31.2 us
    all_gather x1, waiting for transfers between devices, on_device(): normed = lax.all_gather(own_normed, 'head', axis=0, tiled=True)  29.7 us
    all_to_all x1, blocking collectives, from_everyone(): lax.all_to_all(jnp.broadcast_to(array[None], (length, *array.shape)), axi...  17.4 us
    unnamed x66, local copies, waits for them, and re-layouts  10.6 us
    dot_general x1, matrix products, on_device(): jnp.dot(normed, joined_proj, preferred_element_type=jnp.float32)  8.94 us
    dot_general x1, matrix products, on_device(): jnp.dot(normed_out, out_proj, preferred_element_type=jnp.float32)  6.16 us
    dot_general x1, matrix products, on_device(): outer_part = jnp.dot(normed, outer_proj, preferred_element_type=jnp.float32)  5.31 us
  transfers between devices with their start and end apart: 3, of which 2 were waited for; matrix products, arithmetic and copies ran while one was open for 9% of the time, Pallas kernels for 0%

commit v1 on v0

--- a/solution.py
+++ b/solution.py
@@ -8,6 +8,11 @@
 SEQ = ("seq_0", "seq_1")
 SEQ_HEAD = ("seq_0", "seq_1", "head")
 norm_floor = 0.1
+
+
+def gather_by_exchange(value, axis, dim):
+    copies = jnp.concatenate([value] * lax.axis_size(axis), axis=dim)
+    return lax.all_to_all(copies, axis, dim, dim, tiled=True)
 
 
 def passed_along(block, axis, distance):
@@ -99,7 +104,7 @@
     kernel_size = kernel_x.shape[0]
     joined_proj = inner_proj.reshape(model_width, 2 * local_width)
     own_normed = row_norm(tokens, pre_gain).astype(jnp.bfloat16)
-    normed = lax.all_gather(own_normed, "head", axis=0, tiled=True)
+    normed = gather_by_exchange(own_normed, "head", 0)
     inner_part = jnp.dot(normed, joined_proj, preferred_element_type=jnp.float32)
     outer_part = jnp.dot(normed, outer_proj, preferred_element_type=jnp.float32)
     projected = jnp.concatenate([inner_part, outer_part], axis=1)

time: 242 us -> 265 us (1.095)
  waiting for transfers between devices: 33.8 us -> 41.9 us
  starting transfers between devices: 3.23 us -> 9.62 us
  other arithmetic: 28 us -> 32.3 us
    all_to_all x0 -> x1, waiting for transfers between devices: none -> 37.9 us  [gather_by_exchange(): return lax.all_to_all(copies, axis, dim, dim, tiled=True)]
    all_gather x1 -> x0, waiting for transfers between devices: 29.7 us -> none  [on_device(): normed = lax.all_gather(own_normed, 'head', axis=0, tiled=True)]
    all_to_all x0 -> x1, starting transfers between devices: none -> 7.61 us  [gather_by_exchange(): return lax.all_to_all(copies, axis, dim, dim, tiled=True)]
    unnamed x1 -> x8, other arithmetic: 0.6 us -> 4.71 us
  transfers between devices with their start and end apart: 3 -> 3, of which waited for: 2 -> 2; matrix products, arithmetic and copies ran while one was open for 9% -> 8% of each run, Pallas kernels for 0% -> 0%
where the time goes in v1:
time: 265 us; the launch traced here: 264 us
  blocking collectives  100 us (38%)
  waiting for transfers between devices  41.9 us (16%)
  local copies, waits for them, and re-layouts  34 us (13%)
  other arithmetic  32.3 us (12%)
  matrix products  31.9 us (12%)
  between operations  13.9 us (5%)
  starting transfers between devices  9.62 us (4%)
    all_to_all x1, blocking collectives, summed_on_arrival(): lax.all_to_all(pieces, axis, split_axis=0, concat_axis=0, tiled=True)  49.8 us
    all_to_all x1, waiting for transfers between devices, gather_by_exchange(): return lax.all_to_all(copies, axis, dim, dim, tiled=True)  37.9 us
    all_gather x3, blocking collectives, entering(): lax.all_gather(part.astype(kind), axis)  32.9 us
    all_to_all x1, blocking collectives, from_everyone(): lax.all_to_all(jnp.broadcast_to(array[None], (length, *array.shape)), axi...  17.4 us
    unnamed x66, local copies, waits for them, and re-layouts  11.9 us
    dot_general x1, matrix products, on_device(): jnp.dot(normed, joined_proj, preferred_element_type=jnp.float32)  9.95 us
    all_to_all x1, starting transfers between devices, gather_by_exchange(): return lax.all_to_all(copies, axis, dim, dim, tiled=True)  7.61 us
    dot_general x1, matrix products, on_device(): jnp.dot(normed_out, out_proj, preferred_element_type=jnp.float32)  6.16 us
  transfers between devices with their start and end apart: 3, of which 2 were waited for; matrix products, arithmetic and copies ran while one was open for 8% of the time, Pallas kernels for 0%

profile of v1, /device:TPU:1, one launch (start us, length us, event | category | flops | bytes accessed | tf_op | source)
XLA Modules:
  0.0 263.7 jit_solution(6573897375595743703)
XLA Ops:
  6.5 1.4 fusion.16
  7.9 1.2 constant_dynamic-update-slice_fusion.9
  9.2 1.2 constant_dynamic-update-slice_fusion.8
  10.4 0.9 constant_dynamic-update-slice_fusion.7
  12.3 2.0 copy-done.6
  14.3 7.6 %all-to-all-start = ((bf16[8,96,2560]{2,1,0:T(8,128)(2,1)}), bf16[8,96,2560]{2,1,0:T(8,128)(2,1)}, u32[]{:S(2)}, u32[]{:S(2)}) async-start(bf16[8,96,2560]{2,1,0:T(8,128)(2,1)} %bitcast.171), calls=%async_computation | async-start | bytes 7864320 | tf_op jit(solution)/shard_map/all_to_all | solution.py:15
  21.9 6.7 %copy.137 = bf16[320,8,2,640]{3,1,2,0:T(8,128)(2,1)} copy(bf16[320,8,2,640]{3,2,1,0:T(2,128)(2,1)} %bitcast.169) | data formatting | bytes 13107200
  29.9 37.9 %all-to-all-done = bf16[8,96,2560]{2,1,0:T(8,128)(2,1)} async-done(((bf16[8,96,2560]{2,1,0:T(8,128)(2,1)}), bf16[8,96,2560]{2,1,0:T(8,128)(2,1)}, u32[]{:S(2)}, u32[]{:S(2)}) %all-to-all-start) | async-done | bytes 3932192 | tf_op jit(solution)/shard_map/all_to_all | solution.py:15
  67.9 10.0 %convolution_convert_fusion.1 = bf16[768,1280]{1,0:T(8,128)(2,1)} fusion(bf16[768,2560]{1,0:T(8,128)(2,1)} %bitcast.1, bf16[2560,1280]{1,0:T(8,128)(2,1)} %bitcast.170), kind=kOutput, calls=%fused_computation.9 | convolution fusion | flops 5034147840 | bytes 12451840 | tf_op jit(solution)/shard_map/dot_general | solution.py:108
  77.8 4.8 %fusion.66 = (bf16[768,336]{0,1:T(8,128)(2,1)}, f32[768,336]{0,1:T(8,128)}) fusion(bf16[768,2560]{1,0:T(8,128)(2,1)} %bitcast.1, bf16[2560,336]{0,1:T(8,128)(2,1)S(1)} %copy-done.27), kind=kOutput, calls=%fused_computation.152 | convolution fusion | flops 1321463808 | bytes 7200768 | tf_op jit(solution)/shard_map/dot_general | solution.py:109
  82.6 2.1 copy.111
  84.7 1.5 pad_maximum_fusion.2
  86.4 1.2 pad_maximum_fusion.1
  87.6 1.0 slice.213
  88.7 1.7 reduce-window.6
  91.2 2.0 collective-permute-start
  93.9 0.7 copy.124
  95.2 0.7 copy.125
  95.8 5.0 %multiply_convert_fusion.2 = bf16[768,896]{1,0:T(8,128)(2,1)S(1)} fusion(bf16[768,896]{1,0:T(8,128)(2,1)} %pad_maximum_fusion.1, bf16[3,896]{1,0:T(4,128)(2,1)S(1)} %collective-permute-done, f32[896]{0:T(1024)S(1)} %get-tuple-element.6, f32[896]{0:T(1024)S(1)} %get-tuple-element.7, f32[896]{0:T(1024)S(1)} %get-tuple-element.8, f32[896]{0:T(1024)S(1)} %get-tuple-element.5, ...), kind=kLoop, calls=%fused_computation.10 | loop fusion | flops 17891328 | bytes 2775808 | tf_op jit(solution)/shard_map/convert_element_type | solution.py:127
  100.9 0.7 fusion.65
  101.6 1.0 slice.210
  102.6 2.2 copy.112
  104.9 3.8 %reshape.239 = bf16[3,256,10,64]{1,0,3,2:T(4,128)(2,1)} reshape(bf16[768,640]{0,1:T(8,128)(2,1)} %copy.112) | data formatting | bytes 1966080 | tf_op jit(solution)/shard_map/reshape | solution.py:129
  108.6 1.8 fusion.19
  110.4 3.6 %convolution_bitcast_fusion = f32[4,10,64,128]{3,0,2,1:T(4,128)S(1)} fusion(f32[3,10,64,128]{3,2,1,0:T(8,128)S(1)} %fusion.19, f32[10,3]{1,0:T(8,128)} %copy.125, f32[10,4]{1,0:T(8,128)} %copy.124, pred[4,3]{1,0:T(4,128)(4,1)} %iota_compare_fusion.1), kind=kOutput, calls=%fused_computation.26 | convolution fusion | flops 11796840 | bytes 2294052 | tf_op jit(solution)/shard_map/hce,ehpn->chpn/dot_general | solution.py:165
  114.0 1.0 copy-done.3
  115.4 0.7 copy.128
  116.7 1.3 slice_exponential_fusion
  118.1 13.8 %all-gather = bf16[8,1,10]{2,1,0:T(2,128)(2,1)S(1)} all-gather(bf16[1,1,10]{2,1,0:T(2,128)(2,1)S(1)} %slice_bitcast_fusion.5), channel_id=1, replica_groups=mesh['seq_0'=4,'seq_1'=8,'head'=8] {'seq_1'}, dimensions={0}, use_global_device_ids=true | all-gather | bytes 180 | tf_op jit(solution)/shard_map/all_gather | solution.py:36
  133.0 8.4 %all-gather.1 = bf16[4,1,10]{2,1,0:T(2,128)(2,1)} all-gather(bf16[1,1,10]{2,1,0:T(2,128)(2,1)S(1)} %get-tuple-element.17), channel_id=1, replica_groups=mesh['seq_0'=4,'seq_1'=8,'head'=8] {'seq_0'}, dimensions={0}, use_global_device_ids=true | all-gather | bytes 100 | tf_op jit(solution)/shard_map/all_gather | solution.py:36
  142.0 0.8 copy.127
  142.8 1.4 copy.119
  145.4 0.7 fusion.49
  146.1 2.1 fusion.67
  148.2 4.0 %all-gather.4.cloned.1.call-done = bf16[8,10,64,128]{3,2,1,0:T(8,128)(2,1)} async-done(((bf16[1,10,64,128]{3,2,1,0:T(8,128)(2,1)}), bf16[8,10,64,128]{3,2,1,0:T(8,128)(2,1)}) %all-gather.4.cloned.1.call-update) | async-done | bytes 1310736 | tf_op jit(solution)/shard_map/all_gather | solution.py:36
  152.2 1.9 fusion.28
  154.0 10.7 %all_gather.19 = bf16[4,10,64,128]{3,2,1,0:T(8,128)(2,1)S(1)} all-gather(bf16[1,10,64,128]{3,2,1,0:T(8,128)(2,1)S(1)} %fusion.28), channel_id=1, replica_groups=mesh['seq_0'=4,'seq_1'=8,'head'=8] {'seq_0'}, dimensions={0}, use_global_device_ids=true | all-gather | bytes 819200 | tf_op jit(solution)/shard_map/all_gather | solution.py:36
  164.8 2.3 add_bitcast_fusion
  167.6 0.9 fusion.21
  168.7 2.7 %fusion.8 = f32[3,256,10,64]{1,3,2,0:T(8,128)S(1)} fusion(f32[3,256,10,64]{1,3,2,0:T(8,128)S(1)} %fusion.21, f32[3,10,256]{2,1,0:T(8,128)S(1)} %copy-done.13, f32[3,10,256]{2,1,0:T(8,128)S(1)} %copy-done.11, f32[3,256,256]{2,1,0:T(8,128)S(1)} %copy-done.9, pred[256,256]{1,0:T(8,128)(4,1)S(1)} %copy-done.10, f32[10]{0:T(128)S(1)} %copy-done.30, ...), kind=kOutput, calls=%fused_computation.16 | convolution fusion | flops 265912320 | bytes 5859368 | tf_op jit(solution)/shard_map/chts,cshp->cthp/dot_general | solution.py:147
  171.4 1.4 copy.130
  172.8 1.7 copy.138
  174.5 2.9 %copy.131 = f32[768,640]{1,0:T(8,128)} copy(f32[768,640]{0,1:T(8,128)} %bitcast.168) | data formatting | bytes 3932160 | tf_op jit(solution)/shard_map/reshape | solution.py:191
  177.4 2.5 multiply_reduce_fusion
  179.9 17.4 %all_to_all.23 = f32[8,1,768]{2,1,0:T(1,128)S(1)} all-to-all(f32[8,1,768]{2,1,0:T(1,128)S(1)} %broadcast_in_dim.36), channel_id=1, replica_groups=mesh['seq_0'=4,'seq_1'=8,'head'=8] {'head'}, dimensions={0} | all-to-all | bytes 49152 | tf_op jit(solution)/shard_map/all_to_all | solution.py:53
  197.3 6.2 %convolution_convert_fusion = bf16[768,2560]{1,0:T(8,128)(2,1)S(1)} fusion(bf16[640,2560]{1,0:T(8,128)(2,1)S(1)} %copy-done, f32[640]{0:T(1024)S(1)} %copy-done.28, f32[768]{0:T(1024)S(1)} %add_rsqrt_fusion, f32[768,640]{1,0:T(8,128)} %copy.131, bf16[768,1280]{1,0:T(8,128)(2,1)} %convolution_convert_fusion.1), kind=kOutput, calls=%fused_computation.1 | convolution fusion | flops 2522972160 | bytes 10163712 | tf_op jit(solution)/shard_map/dot_general | solution.py:199
  203.5 49.8 %all_to_all.24 = bf16[8,96,2560]{2,1,0:T(8,128)(2,1)} all-to-all(bf16[8,96,2560]{2,1,0:T(8,128)(2,1)S(1)} %bitcast.172), channel_id=1, replica_groups=mesh['seq_0'=4,'seq_1'=8,'head'=8] {'head'}, dimensions={0} | all-to-all | bytes 7864320 | tf_op jit(solution)/shard_map/all_to_all | solution.py:70
  253.3 3.6 %reduce_sum.42 = bf16[96,2560]{1,0:T(8,128)(2,1)} reduce(bf16[8,96,2560]{2,1,0:T(8,128)(2,1)} %all_to_all.24, bf16[]{:T(256)} %constant.60.clone.1), dimensions={0}, to_apply=%region_6.7 | reduce | flops 1720320 | bytes 4423682 | tf_op jit(solution)/shard_map/reduce_sum | solution.py:71
  (106 shorter events, 9.2 us)
Async XLA Ops:
  6.5 190.8 %copy-start = (bf16[640,2560]{1,0:T(8,128)(2,1)S(1)}, bf16[640,2560]{1,0:T(8,128)(2,1)}, u32[]{:S(2)}) copy-start(bf16[640,2560]{1,0:T(8,128)(2,1)} %param.25) | copy-start | bytes 9830404
  6.5 3.9 %copy-start.1 = (bf16[96,2560]{1,0:T(8,128)(2,1)S(1)}, bf16[96,2560]{1,0:T(8,128)(2,1)}, u32[]{:S(2)}) copy-start(bf16[96,2560]{1,0:T(8,128)(2,1)} %param.13) | copy-start | bytes 1474564
  6.5 4.8 %copy-start.8 = (f32[2560]{0:T(1024)S(1)}, f32[2560]{0:T(1024)}, u32[]{:S(2)}) copy-start(f32[2560]{0:T(1024)} %param.14) | copy-start | bytes 30724
  12.3 2.0 copy-start.6
  14.3 53.6 %all-to-all-start = ((bf16[8,96,2560]{2,1,0:T(8,128)(2,1)}), bf16[8,96,2560]{2,1,0:T(8,128)(2,1)}, u32[]{:S(2)}, u32[]{:S(2)}) async-start(bf16[8,96,2560]{2,1,0:T(8,128)(2,1)} %bitcast.171), calls=%async_computation | async-start | bytes 7864320 | tf_op jit(solution)/shard_map/all_to_all | solution.py:15
  21.9 130.3 %all-gather.4.cloned.1.call-start = ((), (), s32[]{:S(2)}) async-start(), calls=%async_computation.3 | async-start | bytes 1474560 | tf_op jit(solution)/shard_map/all_gather | solution.py:36
  21.9 7.4 %copy-start.16 = (f32[4,640]{1,0:T(4,128)S(1)}, f32[4,640]{1,0:T(4,128)}, u32[]{:S(2)}) copy-start(f32[4,640]{1,0:T(4,128)} %param.17) | copy-start | bytes 30724
  21.9 7.4 %copy-start.22 = (f32[4,256]{1,0:T(4,128)S(1)}, f32[4,256]{1,0:T(4,128)}, u32[]{:S(2)}) copy-start(f32[4,256]{1,0:T(4,128)} %param.18) | copy-start | bytes 12292
  21.9 7.4 %copy-start.23 = (f32[640]{0:T(1024)S(1)}, f32[640]{0:T(1024)}, u32[]{:S(2)}) copy-start(f32[640]{0:T(1024)} %param.19) | copy-start | bytes 7684
  21.9 7.4 %copy-start.25 = (f32[256]{0:T(256)S(1)}, f32[256]{0:T(256)}, u32[]{:S(2)}) copy-start(f32[256]{0:T(256)} %param.20) | copy-start | bytes 3076
  21.9 8.0 %copy-start.29 = (f32[10]{0:T(128)S(1)}, f32[10]{0:T(128)}, u32[]{:S(2)}) copy-start(f32[10]{0:T(128)} %param.22) | copy-start | bytes 124
  67.9 10.0 %copy-start.27 = (bf16[2560,336]{0,1:T(8,128)(2,1)S(1)}, bf16[2560,336]{0,1:T(8,128)(2,1)}, u32[]{:S(2)}) copy-start(bf16[2560,336]{0,1:T(8,128)(2,1)} %param.16) | copy-start | bytes 5160964
  84.7 1.6 copy-start.2
  84.7 1.7 copy-start.5
  86.4 2.2 copy-start.26
  91.2 4.7 %copy-start.15 = (f32[3,10]{1,0:T(4,128)}, f32[3,10]{1,0:T(4,128)S(1)}, u32[]{:S(2)}) copy-start(f32[3,10]{1,0:T(4,128)S(1)} %reduce_window_sum.36) | copy-start | bytes 364
  91.2 4.7 %collective-permute-start = (bf16[3,896]{1,0:T(4,128)(2,1)}, bf16[3,896]{1,0:T(4,128)(2,1)S(1)}, u32[]{:S(2)}, u32[]{:S(2)}) collective-permute-start(bf16[3,896]{1,0:T(4,128)(2,1)} %pad_maximum_fusion.2), channel_id=1, source_target_pairs={{0,8},{8,16},{16,24},{24,32},{32,40},{40,48},{48,56},{56,64},{64,7... | collective-permute-start | bytes 16136 | tf_op jit(solution)/shard_map/ppermute | solution.py:21
  113.9 1.1 copy-start.3
  131.8 10.1 %copy-start.14 = (bf16[8,1,10]{2,1,0:T(2,128)(2,1)}, bf16[8,1,10]{2,1,0:T(2,128)(2,1)S(1)}, u32[]{:S(2)}) copy-start(bf16[8,1,10]{2,1,0:T(2,128)(2,1)S(1)} %all-gather) | copy-start | bytes 484
  142.0 22.8 %copy-start.17 = (f32[10]{0:T(128)S(1)}, f32[10]{0:T(128)}, u32[]{:S(2)}) copy-start(f32[10]{0:T(128)} %get-tuple-element.18) | copy-start | bytes 124
  142.0 22.8 %copy-start.18 = (f32[10]{0:T(128)S(1)}, f32[10]{0:T(128)}, u32[]{:S(2)}) copy-start(f32[10]{0:T(128)} %get-tuple-element.19) | copy-start | bytes 124
  142.0 22.8 %copy-start.19 = (f32[10]{0:T(128)S(1)}, f32[10]{0:T(128)}, u32[]{:S(2)}) copy-start(f32[10]{0:T(128)} %get-tuple-element.20) | copy-start | bytes 124
  142.0 22.8 %copy-start.20 = (f32[10]{0:T(128)S(1)}, f32[10]{0:T(128)}, u32[]{:S(2)}) copy-start(f32[10]{0:T(128)} %get-tuple-element.21) | copy-start | bytes 124
  142.0 22.8 %copy-start.21 = (f32[10]{0:T(128)S(1)}, f32[10]{0:T(128)}, u32[]{:S(2)}) copy-start(f32[10]{0:T(128)} %get-tuple-element.22) | copy-start | bytes 124
  144.8 20.0 %copy-start.24 = (f32[10]{0:T(128)S(1)}, f32[10]{0:T(128)}, u32[]{:S(2)}) copy-start(f32[10]{0:T(128)} %get-tuple-element.9) | copy-start | bytes 124
  152.2 15.0 %copy-start.4 = (f32[4,10,64,128]{3,0,2,1:T(4,128)S(1)}, f32[4,10,64,128]{3,0,2,1:T(4,128)}, u32[]{:S(2)}) copy-start(f32[4,10,64,128]{3,0,2,1:T(4,128)} %copy-done.3) | copy-start | bytes 3932164
  167.1 1.4 copy-start.7
  167.1 1.5 copy-start.9
  167.2 1.5 copy-start.10
  167.2 1.5 copy-start.11
  167.2 1.5 copy-start.12
  167.2 1.5 copy-start.13
  167.2 1.5 copy-start.30
  174.5 22.9 %copy-start.28 = (f32[640]{0:T(1024)S(1)}, f32[640]{0:T(1024)}, u32[]{:S(2)}) copy-start(f32[640]{0:T(1024)} %param.24) | copy-start | bytes 7684
Sparse Core Ops, SparseCore 0:
  116.2 35.9 all-gather.3
